TPU v7x, 256 devices: a whole 4x4x8 slice. The times are simulated.
256 devices in a mesh: grp: 8 (over z), mem: 32 (over y, x, core).
Axes of the slice: x: 4, y: 4, z: 8, core: 2. Of those that a mesh axis runs over, the one named last changes fastest.
Arguments:
- child_means: float32 [524288, 64], P(('grp', 'mem')), may hold values from -48 to 48
- child_variances: float32 [524288, 64], P(('grp', 'mem')), may hold values from 0.2 to 2
- virtual_counts: int32 [524288], P(('grp', 'mem')), may hold values from 1 to 4
- assignment: int32 [524288, 1], P(('grp', 'mem')), may hold values from 0 to 511
Outputs:
- parent_means: float32 [512, 64], P('mem')
- parent_variances: float32 [512, 64], P('mem')
- parent_weights: float32 [512], P('mem')
All inputs are finite; a program needn't handle non-finite values.
Results may differ from a plain program's by a relative error of at most 0.0003.
Values sent between devices are 32-bit elements; how exact they have to be, the bound alone decides.
No kernel may reach another device: no remote copies, remote signals or barrier semaphores. Data moves between devices by JAX's collectives and lax.ppermute only.
A program may use at most 64 MiB of HBM per device.

v0:
```python
import math

import jax
import jax.numpy as jnp
from jax import lax
from jax.sharding import Mesh
from jax.sharding import PartitionSpec as P

P_SIZE = 512
ITERS = 2
GRP_MEM = ("grp", "mem_0", "mem_1", "mem_2")
MEM = ("mem_0", "mem_1", "mem_2")


def by_axis(value, axes):
    for axis in axes:
        value = lax.psum(value, axis)
    return value


def cut_along(value, dim, size):
    before, after = (value.shape[:dim], value.shape[dim + 1 :])
    return jnp.moveaxis(value.reshape(*before, size, -1, *after), dim, 0)


def summed_on_arrival(value, axis, dim):
    size = lax.axis_size(axis)
    pieces = lax.all_to_all(cut_along(value, dim, size), axis, 0, 0, tiled=True)
    return jnp.sum(pieces, axis=0)


def in_one_piece(arrays, axis, dim, along):
    columns = [a.reshape(*a.shape[:along], -1) for a in arrays]
    both = jnp.concatenate(columns, axis=along)
    filled, at, done = (summed_on_arrival(both, axis, dim), 0, [])
    for a, column in zip(arrays, columns):
        section = filled[..., at : at + column.shape[along]]
        done.append(section.reshape(*section.shape[:along], *a.shape[along:]))
        at += column.shape[along]
    return tuple(done)


def copy_for_each(value, axis):
    size = lax.axis_size(axis)
    return lax.all_to_all(
        jnp.broadcast_to(value[None], (size, *value.shape)), axis, 0, 0, tiled=True
    )


def taken_together(value, axis):
    return copy_for_each(value, axis).sum(axis=0)


def in_one(arrays, axis):
    ends = [0]
    for a in arrays:
        ends.append(ends[-1] + a.size)
    total = taken_together(jnp.concatenate([a.ravel() for a in arrays]), axis)
    return tuple((total[b:e].reshape(a.shape) for a, b, e in zip(arrays, ends, ends[1:])))


def in_one_piece_2(arrays, axis, dim, along):
    columns = [a.reshape(*a.shape[:along], -1) for a in arrays]
    both = jnp.concatenate(columns, axis=along)
    filled, at, done = (lax.all_gather(both, axis, axis=dim, tiled=True), 0, [])
    for a, column in zip(arrays, columns):
        section = filled[..., at : at + column.shape[along]]
        done.append(section.reshape(*section.shape[:along], *a.shape[along:]))
        at += column.shape[along]
    return tuple(done)


def child_features(means, variances):
    return jnp.concatenate([means, variances + means * means], axis=1)


def accumulate(features, extras, weigh):
    row_count = features.shape[0]
    block = math.gcd(row_count, 1024)
    turns = row_count // block
    pieces = (features.reshape(turns, block, features.shape[1]),) + tuple(
        (extra.reshape((turns, block) + extra.shape[1:]) for extra in extras)
    )

    def advance(carry, piece):
        weights = weigh(*piece)
        sums = carry[0] + lax.dot_general(
            weights,
            piece[0],
            (((0,), (0,)), ((), ())),
            precision=lax.Precision.HIGHEST,
            preferred_element_type=jnp.float32,
        )
        counts = carry[1] + jnp.sum(weights, axis=0)
        return ((sums, counts), None)

    start_sums = (
        jnp.zeros((P_SIZE, features.shape[1]), jnp.float32),
        jnp.zeros((P_SIZE,), jnp.float32),
    )
    return lax.scan(advance, start_sums, pieces)[0]


def maximize(counts, sums, total):
    width = sums.shape[1] // 2
    mass = counts + 1.0
    means = sums[:, :width] / mass[:, None]
    second = (sums[:, width:] + 1.0) / mass[:, None]
    return (means, second - means * means, mass / (total + P_SIZE))


def parent_table(means, variances, weights):
    inverse = 1.0 / variances
    table = jnp.concatenate([-2.0 * means * inverse, inverse], axis=1)
    offset = jnp.sum(jnp.log(2.0 * math.pi * variances) + means * means * inverse, axis=1)
    return (table, offset, jnp.log(weights))


def soft_weights(block_features, block_virtual, table, offset, log_weight):
    width = block_features.shape[1] // 2
    cross = lax.dot_general(
        block_features,
        table,
        (((1,), (1,)), ((), ())),
        precision=lax.Precision.HIGHEST,
        preferred_element_type=jnp.float32,
    )
    ell = -0.5 / width * (cross + offset[None, :])
    score = log_weight[None, :] + block_virtual[:, None] * ell
    top = jnp.max(score, axis=1, keepdims=True)
    expd = jnp.exp(score - top)
    resp = expd / jnp.sum(expd, axis=1, keepdims=True)
    return resp * block_virtual[:, None]


def shards(child_means, child_variances, virtual_counts, assignment):
    features = child_features(child_means, child_variances)
    virtual = virtual_counts.astype(jnp.float32)
    labels = jnp.arange(P_SIZE, dtype=jnp.int32)

    def initial_weights(block_features, block_virtual, block_assign):
        return (block_assign == labels[None, :]).astype(jnp.float32) * block_virtual[:, None]

    sums, counts = accumulate(features, (virtual, assignment), initial_weights)
    total = by_axis(jnp.sum(virtual), GRP_MEM)

    def combine(local_sums, local_counts):
        shared = in_one_piece((local_sums, local_counts), MEM, 0, 1)
        return in_one((shared[0], shared[1]), "grp")

    own_sums, own_counts = combine(sums, counts)
    means, variances, weights = maximize(own_counts, own_sums, total)
    for iteration in range(ITERS):
        all_means, all_variances, all_weights = in_one_piece_2(
            (means, variances, weights), MEM, 0, 1
        )
        table, offset, log_weight = parent_table(all_means, all_variances, all_weights)

        def weigh(block_features, block_virtual):
            return soft_weights(block_features, block_virtual, table, offset, log_weight)

        sums, counts = accumulate(features, (virtual,), weigh)
        own_sums, own_counts = combine(sums, counts)
        means, variances, weights = maximize(own_counts, own_sums, total)
    return (means, variances, weights)


def solution(mesh):
    split = Mesh(
        mesh.devices.reshape(mesh.shape["grp"], 4, 4, 2), ("grp", "mem_0", "mem_1", "mem_2")
    )
    return jax.shard_map(
        shards,
        mesh=split,
        in_specs=(P(GRP_MEM, None), P(GRP_MEM, None), P(GRP_MEM), P(GRP_MEM, None)),
        out_specs=(P(MEM, None), P(MEM, None), P(MEM)),
        check_vma=False,
    )
```

profile of v0, /device:TPU:1, one launch (start us, length us, event | category | flops | bytes accessed | tf_op | source)
XLA Modules:
  0.0 213.9 jit_solution(10653394932134514791)
XLA Ops:
  3.5 8.4 %while.39 = (s32[]{:T(128)}, f32[512,128]{1,0:T(8,128)S(1)}, f32[512]{0:T(512)S(1)}, s32[2,1024,1]{1,2,0:T(1,128)S(1)}, f32[2,1024]{1,0:T(2,128)S(1)}, /*index=5*/f32[2,1024,128]{2,1,0:T(8,128)S(1)}, s32[]{:T(128)}, s32[]{:T(128)}) while((s32[]{:T(128)}, f32[512,128]{1,0:T(8,128)S(1)}, f32[512]{0:T(512)S(1)}, ...), condition=%wide.region_2.3_spmd.clone, body=%wide.region_0.2_spmd.clone.sunk | while | flops 808059392 | bytes 1089644 | solution.py:101
  3.5 3.8 %fusion.57 = f32[512,128]{1,0:T(8,128)S(1)} fusion(f32[1024]{0:T(1024)S(1)} %bitcast.73, s32[1024]{0:T(1024)S(1)} %bitcast.75, f32[2,1024,128]{2,1,0:T(8,128)S(1)} %get-tuple-element.440, s32[]{:T(128)} %get-tuple-element.427, f32[512,128]{1,0:T(8,128)S(1)} %get-tuple-element.428, pred[]{:T(512)S(6)} %compare.9), kind=kOutput, calls=%fused_computation.5.clone.1 | convolution fusion | flops 806486016 | bytes 1056773 | tf_op jit(solution)/shard_map/while/body/eval_jaxpr/dot_general | solution.py:87
  7.7 3.8 %fusion.57 = f32[512,128]{1,0:T(8,128)S(1)} fusion(f32[1024]{0:T(1024)S(1)} %bitcast.73, s32[1024]{0:T(1024)S(1)} %bitcast.75, f32[2,1024,128]{2,1,0:T(8,128)S(1)} %get-tuple-element.440, s32[]{:T(128)} %get-tuple-element.427, f32[512,128]{1,0:T(8,128)S(1)} %get-tuple-element.428, pred[]{:T(512)S(6)} %compare.9), kind=kOutput, calls=%fused_computation.5.clone.1 | convolution fusion | flops 806486016 | bytes 1056773 | tf_op jit(solution)/shard_map/while/body/eval_jaxpr/dot_general | solution.py:87
  12.1 19.8 %all_to_all.33 = f32[32,16,129]{2,1,0:T(8,128)S(1)} all-to-all(f32[32,16,129]{2,1,0:T(8,128)S(1)} %pad_maximum_fusion.1), channel_id=1, replica_groups=mesh['grp'=8,'mem_0'=4,'mem_1'=4,'mem_2'=2] {'mem_0','mem_1','mem_2'}, dimensions={0} | all-to-all | bytes 528384 | tf_op jit(solution)/shard_map/all_to_all | solution.py:28
  32.8 8.2 %all-to-all-start.1 = ((f32[8,1,2064]{2,1,0:T(1,128)}), f32[8,1,2064]{2,1,0:T(1,128)S(1)}, u32[]{:S(2)}, u32[]{:S(2)}) async-start(f32[8,1,2064]{2,1,0:T(1,128)} %broadcast_in_dim.8), calls=%async_computation.1 | async-start | bytes 139264 | tf_op jit(solution)/shard_map/all_to_all | solution.py:45
  41.6 14.2 %psum.28 = f32[]{:T(128)} all-reduce(f32[]{:T(128)} %convert_reduce_fusion), channel_id=1, replica_groups=mesh['grp'=8,'mem_0'=4,'mem_1'=4,'mem_2'=2] {'grp'}, use_global_device_ids=true, to_apply=%region_6.7 | all-reduce | flops 1 | bytes 8 | tf_op jit(solution)/shard_map/psum | solution.py:17
  55.8 7.2 %psum.29 = f32[]{:T(128)} all-reduce(f32[]{:T(128)} %psum.28), channel_id=1, replica_groups=mesh['grp'=8,'mem_0'=4,'mem_1'=4,'mem_2'=2] {'mem_0'}, use_global_device_ids=true, to_apply=%region_7.8 | all-reduce | flops 1 | bytes 8 | tf_op jit(solution)/shard_map/psum | solution.py:17
  63.0 8.1 %psum.30 = f32[]{:T(128)} all-reduce(f32[]{:T(128)} %psum.29), channel_id=1, replica_groups=mesh['grp'=8,'mem_0'=4,'mem_1'=4,'mem_2'=2] {'mem_1'}, use_global_device_ids=true, to_apply=%region_8.9 | all-reduce | flops 1 | bytes 8 | tf_op jit(solution)/shard_map/psum | solution.py:17
  71.0 10.5 %psum.31 = f32[]{:T(128)} all-reduce(f32[]{:T(128)} %psum.30), channel_id=1, replica_groups=mesh['grp'=8,'mem_0'=4,'mem_1'=4,'mem_2'=2] {'mem_2'}, use_global_device_ids=true, to_apply=%region_9.10 | all-reduce | flops 1 | bytes 8 | tf_op jit(solution)/shard_map/psum | solution.py:17
  82.6 23.0 %all_gather.6 = f32[512,129]{1,0:T(8,128)S(1)} all-gather(f32[16,129]{1,0:T(8,128)S(1)} %pad_maximum_fusion.6), channel_id=1, replica_groups=mesh['grp'=8,'mem_0'=4,'mem_1'=4,'mem_2'=2] {'mem_0','mem_1','mem_2'}, dimensions={0}, use_global_device_ids=true | all-gather | bytes 272448 | tf_op jit(solution)/shard_map/all_gather | solution.py:65
  106.1 12.3 %while.40 = (s32[]{:T(128)}, f32[512,128]{1,0:T(8,128)}, f32[512]{0:T(512)S(1)}, f32[512]{0:T(512)S(1)}, f32[2,1024,128]{2,1,0:T(8,128)S(1)}, /*index=5*/f32[512...) while((s32[]{:T(128)}, f32[512,128]{1,0:T(8,128)}, ...), condition=%wide.region_15.16_spmd.clone, body=%wide.region_11.15_spmd.clone.sunk | while | flops 1617559040 | bytes 10293372 | solution.py:101
  106.1 2.0 fusion.60
  109.0 2.7 %convolution_add_fusion.4 = f32[512,128]{1,0:T(8,128)} fusion(f32[2,1024,128]{2,1,0:T(8,128)S(1)} %get-tuple-element.467, s32[]{:T(128)} %get-tuple-element.453, f32[1024,512]{0,1:T(8,128)S(1)} %get-tuple-element.407, f32[1024]{0:T(1024)S(1)} %bitcast.69, f32[1024]{0:T(1024)S(1)} %fusion.61, f32[1024]{0:T(1024)S(1)} %get-tuple-element.408, ...), kind=kOutput, calls=%fused_computation.20.clone.1 | convolution fusion | flops 807010304 | bytes 3158021 | tf_op jit(solution)/shard_map/while/body/eval_jaxpr/dot_general | solution.py:87
  111.8 2.0 fusion.60
  114.7 3.7 %convolution_add_fusion.4 = f32[512,128]{1,0:T(8,128)} fusion(f32[2,1024,128]{2,1,0:T(8,128)S(1)} %get-tuple-element.467, s32[]{:T(128)} %get-tuple-element.453, f32[1024,512]{0,1:T(8,128)S(1)} %get-tuple-element.407, f32[1024]{0:T(1024)S(1)} %bitcast.69, f32[1024]{0:T(1024)S(1)} %fusion.61, f32[1024]{0:T(1024)S(1)} %get-tuple-element.408, ...), kind=kOutput, calls=%fused_computation.20.clone.1 | convolution fusion | flops 807010304 | bytes 3158021 | tf_op jit(solution)/shard_map/while/body/eval_jaxpr/dot_general | solution.py:87
  119.5 16.1 %all_to_all.34 = f32[32,16,129]{2,1,0:T(8,128)S(1)} all-to-all(f32[32,16,129]{2,1,0:T(8,128)S(1)} %pad_maximum_fusion.2), channel_id=1, replica_groups=mesh['grp'=8,'mem_0'=4,'mem_1'=4,'mem_2'=2] {'mem_0','mem_1','mem_2'}, dimensions={0} | all-to-all | bytes 528384 | tf_op jit(solution)/shard_map/all_to_all | solution.py:28
  136.5 4.3 %all-to-all-start.3 = ((f32[8,1,2064]{2,1,0:T(1,128)}), f32[8,1,2064]{2,1,0:T(1,128)S(1)}, u32[]{:S(2)}, u32[]{:S(2)}) async-start(f32[8,1,2064]{2,1,0:T(1,128)} %broadcast_in_dim.9), calls=%async_computation.3 | async-start | bytes 139264 | tf_op jit(solution)/shard_map/all_to_all | solution.py:45
  140.7 7.2 %all-to-all-done.3 = f32[8,1,2064]{2,1,0:T(1,128)S(1)} async-done(((f32[8,1,2064]{2,1,0:T(1,128)}), f32[8,1,2064]{2,1,0:T(1,128)S(1)}, u32[]{:S(2)}, u32[]{:S(2)}) %all-to-all-start.3) | async-done | bytes 66080 | tf_op jit(solution)/shard_map/all_to_all | solution.py:45
  148.2 24.9 %all_gather.7 = f32[512,129]{1,0:T(8,128)S(1)} all-gather(f32[16,129]{1,0:T(8,128)S(1)} %pad_maximum_fusion.7), channel_id=1, replica_groups=mesh['grp'=8,'mem_0'=4,'mem_1'=4,'mem_2'=2] {'mem_0','mem_1','mem_2'}, dimensions={0}, use_global_device_ids=true | all-gather | bytes 272448 | tf_op jit(solution)/shard_map/all_gather | solution.py:65
  173.7 12.3 %while.41 = (s32[]{:T(128)}, f32[512,128]{1,0:T(8,128)}, f32[512]{0:T(512)S(1)}, f32[512]{0:T(512)S(1)}, f32[2,1024,128]{2,1,0:T(8,128)S(1)}, /*index=5*/f32[512...) while((s32[]{:T(128)}, f32[512,128]{1,0:T(8,128)}, ...), condition=%wide.region_23.24_spmd.clone, body=%wide.region_19.23_spmd.clone.sunk | while | flops 1617559040 | bytes 10293372 | solution.py:101
  176.7 2.7 %convolution_add_fusion.5 = f32[512,128]{1,0:T(8,128)} fusion(f32[2,1024,128]{2,1,0:T(8,128)S(1)} %get-tuple-element.497, s32[]{:T(128)} %get-tuple-element.483, f32[1024,512]{0,1:T(8,128)S(1)} %get-tuple-element.417, f32[1024]{0:T(1024)S(1)} %bitcast.72, f32[1024]{0:T(1024)S(1)} %fusion.66, f32[1024]{0:T(1024)S(1)} %get-tuple-element.418, ...), kind=kOutput, calls=%fused_computation.35.clone.1 | convolution fusion | flops 807010304 | bytes 3158021 | tf_op jit(solution)/shard_map/while/body/eval_jaxpr/dot_general | solution.py:87
  182.3 3.7 %convolution_add_fusion.5 = f32[512,128]{1,0:T(8,128)} fusion(f32[2,1024,128]{2,1,0:T(8,128)S(1)} %get-tuple-element.497, s32[]{:T(128)} %get-tuple-element.483, f32[1024,512]{0,1:T(8,128)S(1)} %get-tuple-element.417, f32[1024]{0:T(1024)S(1)} %bitcast.72, f32[1024]{0:T(1024)S(1)} %fusion.66, f32[1024]{0:T(1024)S(1)} %get-tuple-element.418, ...), kind=kOutput, calls=%fused_computation.35.clone.1 | convolution fusion | flops 807010304 | bytes 3158021 | tf_op jit(solution)/shard_map/while/body/eval_jaxpr/dot_general | solution.py:87
  187.2 15.7 %all_to_all.35 = f32[32,16,129]{2,1,0:T(8,128)S(1)} all-to-all(f32[32,16,129]{2,1,0:T(8,128)S(1)} %pad_maximum_fusion.3), channel_id=1, replica_groups=mesh['grp'=8,'mem_0'=4,'mem_1'=4,'mem_2'=2] {'mem_0','mem_1','mem_2'}, dimensions={0} | all-to-all | bytes 528384 | tf_op jit(solution)/shard_map/all_to_all | solution.py:28
  203.1 9.6 %all_to_all.36 = f32[8,1,2064]{2,1,0:T(1,128)S(1)} all-to-all(f32[8,1,2064]{2,1,0:T(1,128)S(1)} %broadcast_in_dim.10), channel_id=1, replica_groups=mesh['grp'=8,'mem_0'=4,'mem_1'=4,'mem_2'=2] {'grp'}, dimensions={0} | all-to-all | bytes 132096 | tf_op jit(solution)/shard_map/all_to_all | solution.py:45
  (90 shorter events, 19.1 us)
Async XLA Ops:
  1.9 1.5 copy-start.1
  1.9 1.5 copy-start
  32.8 49.4 %all-to-all-start.1 = ((f32[8,1,2064]{2,1,0:T(1,128)}), f32[8,1,2064]{2,1,0:T(1,128)S(1)}, u32[]{:S(2)}, u32[]{:S(2)}) async-start(f32[8,1,2064]{2,1,0:T(1,128)} %broadcast_in_dim.8), calls=%async_computation.1 | async-start | bytes 139264 | tf_op jit(solution)/shard_map/all_to_all | solution.py:45
  136.5 11.5 %all-to-all-start.3 = ((f32[8,1,2064]{2,1,0:T(1,128)}), f32[8,1,2064]{2,1,0:T(1,128)S(1)}, u32[]{:S(2)}, u32[]{:S(2)}) async-start(f32[8,1,2064]{2,1,0:T(1,128)} %broadcast_in_dim.9), calls=%async_computation.3 | async-start | bytes 139264 | tf_op jit(solution)/shard_map/all_to_all | solution.py:45
where the time goes:
time: 215 us; the launch traced here: 214 us
  blocking collectives  149 us (69%)
  matrix products  28.5 us (13%)
  starting transfers between devices  12.4 us (6%)
  other arithmetic  11.8 us (5%)
  waiting for transfers between devices  7.2 us (3%)
  local copies, waits for them, and re-layouts  3.24 us (2%)
    all_to_all x3, blocking collectives, summed_on_arrival(): pieces = lax.all_to_all(cut_along(value, dim, size), axis, 0, 0, tiled=True)  51.6 us
    all_gather x2, blocking collectives, in_one_piece_2(): filled, at, done = (lax.all_gather(both, axis, axis=dim, tiled=True), 0, [])  47.9 us
    psum x4, blocking collectives, by_axis(): value = lax.psum(value, axis)  40 us
    dot_general x6, matrix products, advance(): lax.dot_general(weights, piece[0], (((0,), (0,)), ((), ())), precision=la...  20.3 us
    all_to_all x2, starting transfers between devices, copy_for_each(): lax.all_to_all(jnp.broadcast_to(value[None], (size, *value.shape)), axis,...  12.4 us
    all_to_all x1, blocking collectives, copy_for_each(): lax.all_to_all(jnp.broadcast_to(value[None], (size, *value.shape)), axis,...  9.55 us
    dot_general x4, matrix products, soft_weights(): lax.dot_general(block_features, table, (((1,), (1,)), ((), ())), precisio...  8.19 us
    all_to_all x2, waiting for transfers between devices, copy_for_each(): lax.all_to_all(jnp.broadcast_to(value[None], (size, *value.shape)), axis,...  7.2 us
  transfers between devices with their start and end apart: 2, of which 1 were waited for; matrix products, arithmetic and copies ran while one was open for 0% of the time, Pallas kernels for 0%

commit v1 on v0

v1 whole, which is shorter than its diff:
```python
import math

import jax
import jax.numpy as jnp
from jax import lax
from jax.experimental import pallas as pl
from jax.experimental.pallas import tpu as pltpu
from jax.sharding import Mesh
from jax.sharding import PartitionSpec as P

D = 64
P_SIZE = 512
ITERS = 2
MEM_SIZE = 32
OWN = P_SIZE // MEM_SIZE
PIECE = OWN + 1
TILE = 256
GRP_MEM = ("grp", "mem_0", "mem_1", "mem_2")
MEM = ("mem_0", "mem_1", "mem_2")
LOG2E = math.log2(math.e)


def in_two(value):
    high = value.astype(jnp.bfloat16)
    return high, (value - high.astype(jnp.float32)).astype(jnp.bfloat16)


def write_pieces(sums, counts, local_total, out_ref):
    lane = lax.broadcasted_iota(jnp.int32, (OWN, 128), 1)
    row = lax.broadcasted_iota(jnp.int32, (OWN, 128), 0)
    last = lax.broadcasted_iota(jnp.int32, (1, 128), 1) == OWN
    for m in range(MEM_SIZE):
        own = slice(m * OWN, (m + 1) * OWN)
        out_ref[m * PIECE : m * PIECE + OWN, :] = sums[own]
        spread = jnp.where(lane == row, counts[own], 0.0)
        flat = jnp.sum(spread, axis=0, keepdims=True)
        out_ref[m * PIECE + OWN : (m + 1) * PIECE, :] = jnp.where(last, local_total, flat)


def first_kernel(mean_ref, var_ref, virt_ref, label_ref, feat_ref, out_ref, acc_ref, cnt_ref):
    n = mean_ref.shape[0]
    for t in range(n // TILE):
        rows = slice(t * TILE, (t + 1) * TILE)
        mean = mean_ref[rows, :]
        feats = jnp.concatenate([mean, var_ref[rows, :] + mean * mean], axis=1)
        high, low = in_two(feats)
        feat_ref[rows, :128] = high
        feat_ref[rows, 128:] = low
        parent = lax.broadcasted_iota(jnp.int32, (P_SIZE, TILE), 0)
        virt = virt_ref[:, rows].astype(jnp.float32)
        w = jnp.where(parent == label_ref[:, rows], virt, 0.0)
        part = jnp.dot(
            w.astype(jnp.bfloat16), feat_ref[rows, :], preferred_element_type=jnp.float32
        )
        seen = w[:, :128] + w[:, 128:]
        if t == 0:
            acc_ref[...] = part
            cnt_ref[...] = seen
        else:
            acc_ref[...] += part
            cnt_ref[...] += seen
    finish(virt_ref, acc_ref, cnt_ref, out_ref)


def finish(virt_ref, acc_ref, cnt_ref, out_ref):
    local_total = jnp.sum(virt_ref[...].astype(jnp.float32), axis=1, keepdims=True)
    counts = jnp.sum(cnt_ref[...], axis=1, keepdims=True)
    write_pieces(acc_ref[:, :128] + acc_ref[:, 128:], counts, local_total, out_ref)


def step_kernel(table_ref, feat_ref, virt_ref, out_ref, tab_ref, off_ref, score_ref, w_ref, acc_ref, cnt_ref):
    n = feat_ref.shape[0]
    lane = lax.broadcasted_iota(jnp.int32, (OWN, 128), 1)
    row = lax.broadcasted_iota(jnp.int32, (OWN, 128), 0)
    for m in range(MEM_SIZE):
        own = slice(m * OWN, (m + 1) * OWN)
        high, low = in_two(table_ref[m * PIECE : m * PIECE + OWN, :])
        tab_ref[own, 0:128] = high
        tab_ref[own, 128:256] = high
        tab_ref[own, 256:384] = low
        tab_ref[own, 384:512] = low
        extra = jnp.broadcast_to(table_ref[m * PIECE + OWN : (m + 1) * PIECE, :], (OWN, 128))
        for k in range(2):
            column = jnp.sum(jnp.where(lane == row + k * OWN, extra, 0.0), axis=1, keepdims=True)
            off_ref[own, k * 128 : (k + 1) * 128] = jnp.broadcast_to(column, (OWN, 128))
    for t in range(n // TILE):
        rows = slice(t * TILE, (t + 1) * TILE)
        slot = t % 2
        feats = feat_ref[rows, :]
        twice = jnp.concatenate([feats, feats], axis=1)
        cross = lax.dot_general(
            tab_ref[...], twice, (((1,), (1,)), ((), ())), preferred_element_type=jnp.float32
        )
        virt = virt_ref[:, rows].astype(jnp.float32)
        for h in range(TILE // 128):
            half = slice(h * 128, (h + 1) * 128)
            v = virt[:, half]
            score = (cross[:, half] + off_ref[:, :128]) * v + off_ref[:, 128:]
            score_ref[slot, :, half] = score
        score = score_ref[slot]
        top = jnp.max(score, axis=0, keepdims=True)
        expd = jnp.exp2(score - top)
        ratio = virt / jnp.sum(expd, axis=0, keepdims=True)
        w = expd * ratio
        high, low = in_two(w)
        w_ref[slot, :, :TILE] = high
        w_ref[slot, :, TILE:] = low
        part = jnp.dot(
            w_ref[slot], jnp.concatenate([feats, feats], axis=0), preferred_element_type=jnp.float32
        )
        seen = w[:, :128] + w[:, 128:]
        if t == 0:
            acc_ref[...] = part
            cnt_ref[...] = seen
        else:
            acc_ref[...] += part
            cnt_ref[...] += seen
    finish(virt_ref, acc_ref, cnt_ref, out_ref)


def vmem(k):
    return [pl.BlockSpec(memory_space=pltpu.VMEM)] * k


def first_statistics(means, variances, virt, labels, **kw):
    n = means.shape[0]
    return pl.pallas_call(
        first_kernel,
        out_shape=(
            jax.ShapeDtypeStruct((n, 256), jnp.bfloat16),
            jax.ShapeDtypeStruct((MEM_SIZE * PIECE, 128), jnp.float32),
        ),
        in_specs=vmem(4),
        out_specs=tuple(vmem(2)),
        scratch_shapes=[pltpu.VMEM((P_SIZE, 256), jnp.float32), pltpu.VMEM((P_SIZE, 128), jnp.float32)],
        name="first",
        **kw,
    )(means, variances, virt, labels)


def step_statistics(table, feats, virt, **kw):
    return pl.pallas_call(
        step_kernel,
        out_shape=jax.ShapeDtypeStruct((MEM_SIZE * PIECE, 128), jnp.float32),
        in_specs=vmem(3),
        out_specs=vmem(1)[0],
        scratch_shapes=[
            pltpu.VMEM((P_SIZE, 512), jnp.bfloat16),
            pltpu.VMEM((P_SIZE, 256), jnp.float32),
            pltpu.VMEM((2, P_SIZE, TILE), jnp.float32),
            pltpu.VMEM((2, P_SIZE, 2 * TILE), jnp.bfloat16),
            pltpu.VMEM((P_SIZE, 256), jnp.float32),
            pltpu.VMEM((P_SIZE, 128), jnp.float32),
        ],
        name="step",
        **kw,
    )(table, feats, virt)


def reduce_own(pieces):
    size = lax.axis_size("grp")
    arrived = lax.all_to_all(pieces.reshape(MEM_SIZE, 1, PIECE * 128), MEM, 0, 0, tiled=True)
    shared = jnp.sum(arrived, axis=0, keepdims=True)
    copies = lax.all_to_all(
        jnp.broadcast_to(shared, (size, 1, PIECE * 128)), "grp", 0, 0, tiled=True
    )
    return jnp.sum(copies, axis=(0, 1))


def maximize(own):
    sums = own[: OWN * 128].reshape(OWN, 128)
    mass = own[OWN * 128 : OWN * 128 + OWN] + 1.0
    total = own[OWN * 128 + OWN]
    means = sums[:, :D] / mass[:, None]
    second = (sums[:, D:] + 1.0) / mass[:, None]
    return means, second - means * means, mass / (total + P_SIZE)


def parent_table(means, variances, weights):
    scale = -0.5 / D * LOG2E
    inverse = scale / variances
    table = jnp.concatenate([-2.0 * means * inverse, inverse], axis=1)
    offset = jnp.sum(scale * jnp.log(2.0 * math.pi * variances) + means * means * inverse, axis=1)
    extra = jnp.concatenate([offset, LOG2E * jnp.log(weights), jnp.zeros((128 - 2 * OWN,), jnp.float32)])
    piece = jnp.concatenate([table.reshape(-1), extra])
    gathered = lax.all_to_all(
        jnp.broadcast_to(piece[None, None], (MEM_SIZE, 1, PIECE * 128)), MEM, 0, 0, tiled=True
    )
    return gathered.reshape(MEM_SIZE * PIECE, 128)


def shards(child_means, child_variances, virtual_counts, assignment):
    virt = virtual_counts.reshape(1, -1)
    feats, pieces = first_statistics(child_means, child_variances, virt, assignment.reshape(1, -1))
    means, variances, weights = maximize(reduce_own(pieces))
    for iteration in range(ITERS):
        table = parent_table(means, variances, weights)
        pieces = step_statistics(table, feats, virt)
        means, variances, weights = maximize(reduce_own(pieces))
    return (means, variances, weights)


def solution(mesh):
    split = Mesh(
        mesh.devices.reshape(mesh.shape["grp"], 4, 4, 2), ("grp", "mem_0", "mem_1", "mem_2")
    )
    return jax.shard_map(
        shards,
        mesh=split,
        in_specs=(P(GRP_MEM, None), P(GRP_MEM, None), P(GRP_MEM), P(GRP_MEM, None)),
        out_specs=(P(MEM, None), P(MEM, None), P(MEM)),
        check_vma=False,
    )
```

time: 215 us -> 132 us (0.61)
  blocking collectives: 149 us -> 106 us
  matrix products: 28.5 us -> 0 us
  Pallas kernels: 0 us -> 14.4 us
  starting transfers between devices: 12.4 us -> 0 us
  other arithmetic: 11.8 us -> 2.61 us
  waiting for transfers between devices: 7.2 us -> 0 us
  local copies, waits for them, and re-layouts: 3.24 us -> 6.13 us
    all_gather x2 -> x0, blocking collectives: 47.9 us -> none  [in_one_piece_2(): filled, at, done = (lax.all_gather(both, axis, axis=dim, tiled=True), 0, [])]
    all_to_all x4 -> x8, blocking collectives: 61.1 us -> 106 us  [the longest x3 43.2 us: reduce_own(): lax.all_to_all(pieces.reshape(MEM_SIZE, 1, PIECE * 128), MEM, 0, 0, tiled...]
    psum x4 -> x0, blocking collectives: 40 us -> none  [by_axis(): value = lax.psum(value, axis)]
    dot_general x10 -> x0, matrix products: 28.5 us -> none  [the longest x6 20.3 us: advance(): lax.dot_general(weights, piece[0], (((0,), (0,)), ((), ())), precision=la...]
    pallas_call x0 -> x3, Pallas kernels: none -> 14.4 us  [the longest x2 10.9 us: step_statistics(): pl.pallas_call(step_kernel, out_shape=jax.ShapeDtypeStruct((MEM_SIZE * PI...]
    all_to_all x2 -> x0, starting transfers between devices: 12.4 us -> none  [copy_for_each(): lax.all_to_all(jnp.broadcast_to(value[None], (size, *value.shape)), axis,...]
    all_to_all x2 -> x0, waiting for transfers between devices: 7.2 us -> none  [copy_for_each(): lax.all_to_all(jnp.broadcast_to(value[None], (size, *value.shape)), axis,...]
    reduce_sum x19 -> x8, other arithmetic: 5.44 us -> 1.08 us  [the longest x3 0.51 us: reduce_own(): shared = jnp.sum(arrived, axis=0, keepdims=True)]
  transfers between devices with their start and end apart: 2 -> 0, of which waited for: 1 -> 0; matrix products, arithmetic and copies ran while one was open for 0% -> 0% of each run, Pallas kernels for 0% -> 0%
where the time goes in v1:
time: 132 us
  blocking collectives  106 us (80%)
  Pallas kernels  14.4 us (11%)
  local copies, waits for them, and re-layouts  6.13 us (5%)
  between operations  2.68 us (2%)
  other arithmetic  2.61 us (2%)
    all_to_all x3, blocking collectives, reduce_own(): lax.all_to_all(pieces.reshape(MEM_SIZE, 1, PIECE * 128), MEM, 0, 0, tiled...  43.2 us
    all_to_all x3, blocking collectives, reduce_own(): lax.all_to_all(jnp.broadcast_to(shared, (size, 1, PIECE * 128)), 'grp', 0...  34.4 us
    all_to_all x2, blocking collectives, parent_table(): lax.all_to_all(jnp.broadcast_to(piece[None, None], (MEM_SIZE, 1, PIECE *...  28.1 us
    pallas_call x2, Pallas kernels, step_statistics(): pl.pallas_call(step_kernel, out_shape=jax.ShapeDtypeStruct((MEM_SIZE * PI...  10.9 us
    unnamed x4, local copies, waits for them, and re-layouts  3.8 us
    pallas_call x1, Pallas kernels, first_statistics(): pl.pallas_call(first_kernel, out_shape=(jax.ShapeDtypeStruct((n, 256), jn...  3.46 us

profile of v1, /device:TPU:1, one launch (start us, length us, event | category | flops | bytes accessed | tf_op | source)
XLA Modules:
  0.0 131.6 jit_solution(320199131351189639)
XLA Ops:
  0.6 2.5 %copy.19.mean_ref = f32[2048,64]{1,0:T(8,128)} copy(f32[2048,64]{0,1:T(8,128)} %param.4) | data formatting | bytes 1048576 | tf_op args[0]
  3.1 1.3 %copy.20.var_ref = f32[2048,64]{1,0:T(8,128)} copy(f32[2048,64]{0,1:T(8,128)S(1)} %copy-done) | data formatting | bytes 1048576 | tf_op args[1]
  4.4 3.5 %first.1 = (bf16[2048,256]{1,0:T(8,128)(2,1)}, f32[544,128]{1,0:T(8,128)}) custom-call(f32[2048,64]{1,0:T(8,128)} %copy.19.mean_ref, f32[2048,64]{1,0:T(8,128)} %copy.20.var_ref, s32[1,2048]{1,0:T(1,128)} %bitcast.25, s32[1,2048]{1,0:T(1,128)} %bitcast.28), custom_call_target="tpu_custom_call" | custom-call | tf_op jit(solution)/shard_map/first/pallas_call | solution.py:127
  7.9 17.6 %all_to_all.40 = f32[32,1,2176]{2,1,0:T(1,128)S(1)} all-to-all(f32[32,1,2176]{2,1,0:T(1,128)} %bitcast.24), channel_id=1, replica_groups=mesh['grp'=8,'mem_0'=4,'mem_1'=4,'mem_2'=2] {'mem_0','mem_1','mem_2'}, dimensions={0} | all-to-all | bytes 557056 | tf_op jit(solution)/shard_map/all_to_all | solution.py:162
  25.5 0.2 reduce_sum.72
  25.7 15.2 %all_to_all.41 = f32[8,1,2176]{2,1,0:T(1,128)S(1)} all-to-all(f32[8,1,2176]{2,1,0:T(1,128)S(1)} %broadcast_in_dim.10), channel_id=1, replica_groups=mesh['grp'=8,'mem_0'=4,'mem_1'=4,'mem_2'=2] {'grp'}, dimensions={0} | all-to-all | bytes 139264 | tf_op jit(solution)/shard_map/all_to_all | solution.py:164
  40.9 0.6 slice.97
  42.2 0.2 add_reduce_fusion.1
  42.8 14.2 %all_to_all.42 = f32[32,1,2176]{2,1,0:T(1,128)} all-to-all(f32[32,1,2176]{2,1,0:T(1,128)S(1)} %broadcast_in_dim.11), channel_id=1, replica_groups=mesh['grp'=8,'mem_0'=4,'mem_1'=4,'mem_2'=2] {'mem_0','mem_1','mem_2'}, dimensions={0} | all-to-all | bytes 557056 | tf_op jit(solution)/shard_map/all_to_all | solution.py:186
  57.0 5.5 %step.2 = f32[544,128]{1,0:T(8,128)} custom-call(f32[544,128]{1,0:T(8,128)} %bitcast.20, bf16[2048,256]{1,0:T(8,128)(2,1)} %get-tuple-element.6.feat_ref, s32[1,2048]{1,0:T(1,128)} %bitcast.26), custom_call_target="tpu_custom_call" | custom-call | tf_op jit(solution)/shard_map/step/pallas_call | solution.py:142
  62.5 12.8 %all_to_all.43 = f32[32,1,2176]{2,1,0:T(1,128)S(1)} all-to-all(f32[32,1,2176]{2,1,0:T(1,128)} %bitcast.23), channel_id=1, replica_groups=mesh['grp'=8,'mem_0'=4,'mem_1'=4,'mem_2'=2] {'mem_0','mem_1','mem_2'}, dimensions={0} | all-to-all | bytes 557056 | tf_op jit(solution)/shard_map/all_to_all | solution.py:162
  75.3 0.2 reduce_sum.75
  75.5 9.6 %all_to_all.44 = f32[8,1,2176]{2,1,0:T(1,128)S(1)} all-to-all(f32[8,1,2176]{2,1,0:T(1,128)S(1)} %broadcast_in_dim.12), channel_id=1, replica_groups=mesh['grp'=8,'mem_0'=4,'mem_1'=4,'mem_2'=2] {'grp'}, dimensions={0} | all-to-all | bytes 139264 | tf_op jit(solution)/shard_map/all_to_all | solution.py:164
  85.2 0.6 slice.102
  86.4 0.2 add_reduce_fusion
  86.9 0.2 broadcast_in_dim.13
  87.0 13.9 %all_to_all.45 = f32[32,1,2176]{2,1,0:T(1,128)} all-to-all(f32[32,1,2176]{2,1,0:T(1,128)S(1)} %broadcast_in_dim.13), channel_id=1, replica_groups=mesh['grp'=8,'mem_0'=4,'mem_1'=4,'mem_2'=2] {'mem_0','mem_1','mem_2'}, dimensions={0} | all-to-all | bytes 557056 | tf_op jit(solution)/shard_map/all_to_all | solution.py:186
  101.0 5.5 %step.3 = f32[544,128]{1,0:T(8,128)} custom-call(f32[544,128]{1,0:T(8,128)} %bitcast.21, bf16[2048,256]{1,0:T(8,128)(2,1)} %get-tuple-element.6.feat_ref, s32[1,2048]{1,0:T(1,128)} %bitcast.27), custom_call_target="tpu_custom_call" | custom-call | tf_op jit(solution)/shard_map/step/pallas_call | solution.py:142
  106.4 12.8 %all_to_all.46 = f32[32,1,2176]{2,1,0:T(1,128)S(1)} all-to-all(f32[32,1,2176]{2,1,0:T(1,128)} %bitcast.22), channel_id=1, replica_groups=mesh['grp'=8,'mem_0'=4,'mem_1'=4,'mem_2'=2] {'mem_0','mem_1','mem_2'}, dimensions={0} | all-to-all | bytes 557056 | tf_op jit(solution)/shard_map/all_to_all | solution.py:162
  119.2 0.2 reduce_sum.78
  119.5 9.6 %all_to_all.47 = f32[8,1,2176]{2,1,0:T(1,128)S(1)} all-to-all(f32[8,1,2176]{2,1,0:T(1,128)S(1)} %broadcast_in_dim.14), channel_id=1, replica_groups=mesh['grp'=8,'mem_0'=4,'mem_1'=4,'mem_2'=2] {'grp'}, dimensions={0} | all-to-all | bytes 139264 | tf_op jit(solution)/shard_map/all_to_all | solution.py:164
  129.1 0.6 slice.107
  130.4 0.5 broadcast_divide_fusion.2
  130.9 0.7 fusion.1
  (21 shorter events, 0.9 us)
Async XLA Ops:
  0.6 2.5 %copy-start = (f32[2048,64]{0,1:T(8,128)S(1)}, f32[2048,64]{0,1:T(8,128)}, u32[]{:S(2)}) copy-start(f32[2048,64]{0,1:T(8,128)} %param.5) | copy-start | bytes 1572868

commit v2 on v1

v2 whole, which is shorter than its diff:
```python
import math

import jax
import jax.numpy as jnp
from jax import lax
from jax.experimental import pallas as pl
from jax.experimental.pallas import tpu as pltpu
from jax.sharding import Mesh
from jax.sharding import PartitionSpec as P

D = 64
P_SIZE = 512
ITERS = 2
MEM_SIZE = 32
OWN = P_SIZE // MEM_SIZE
PIECE = OWN + 1
TILE = 256
GRP_MEM = ("grp", "mem_0", "mem_1", "mem_2")
MEM = ("mem_0", "mem_1", "mem_2")
LOG2E = math.log2(math.e)
CONTRACT_LANES = (((1,), (1,)), ((), ()))


def in_two(value):
    high = value.astype(jnp.bfloat16)
    return high, (value - high.astype(jnp.float32)).astype(jnp.bfloat16)


def write_pieces(sums, counts, local_total, out_ref):
    lane = lax.broadcasted_iota(jnp.int32, (OWN, 128), 1)
    row = lax.broadcasted_iota(jnp.int32, (OWN, 128), 0)
    last = lax.broadcasted_iota(jnp.int32, (1, 128), 1) == OWN
    for m in range(MEM_SIZE):
        own = slice(m * OWN, (m + 1) * OWN)
        out_ref[m * PIECE : m * PIECE + OWN, :] = sums[own]
        spread = jnp.where(lane == row, counts[own], 0.0)
        flat = jnp.sum(spread, axis=0, keepdims=True)
        out_ref[m * PIECE + OWN : (m + 1) * PIECE, :] = jnp.where(last, local_total, flat)


def first_kernel(
    mean_hbm, var_hbm, virt_hbm, label_hbm, feat_ref, out_ref,
    mean_ref, var_ref, virt_ref, label_ref, acc_ref, cnt_ref, sem
):
    n = mean_ref.shape[1]
    copies = [
        pltpu.make_async_copy(source, target, sem.at[k])
        for k, (source, target) in enumerate(
            (
                (label_hbm, label_ref),
                (virt_hbm, virt_ref),
                (mean_hbm, mean_ref),
                (var_hbm, var_ref),
            )
        )
    ]
    for copy in copies:
        copy.start()
    for copy in copies[:2]:
        copy.wait()
    for t in range(n // TILE):
        rows = slice(t * TILE, (t + 1) * TILE)
        virt = virt_ref[:, rows].astype(jnp.float32)
        parent = lax.broadcasted_iota(jnp.int32, (P_SIZE, TILE), 0)
        w = jnp.where(parent == label_ref[:, rows], virt, 0.0)
        if t == 0:
            for copy in copies[2:]:
                copy.wait()
        mean = mean_ref[:, rows]
        high, low = in_two(jnp.concatenate([mean, var_ref[:, rows] + mean * mean], axis=0))
        feats = jnp.concatenate([high, low], axis=0)
        feat_ref[:, rows] = feats
        part = lax.dot_general(
            w.astype(jnp.bfloat16), feats, CONTRACT_LANES, preferred_element_type=jnp.float32
        )
        add_up(t, part, w, acc_ref, cnt_ref)
    finish(virt_ref, acc_ref, cnt_ref, out_ref)


def add_up(t, part, w, acc_ref, cnt_ref):
    seen = w[:, :128] + w[:, 128:]
    if t == 0:
        acc_ref[...] = part
        cnt_ref[...] = seen
    else:
        acc_ref[...] += part
        cnt_ref[...] += seen


def finish(virt_ref, acc_ref, cnt_ref, out_ref):
    local_total = jnp.sum(virt_ref[...].astype(jnp.float32), axis=1, keepdims=True)
    counts = jnp.sum(cnt_ref[...], axis=1, keepdims=True)
    write_pieces(acc_ref[:, :128] + acc_ref[:, 128:], counts, local_total, out_ref)


def step_kernel(table_ref, feat_ref, virt_ref, out_ref, tab_ref, off_ref, score_ref, w_ref, acc_ref, cnt_ref):
    n = feat_ref.shape[1]
    lane = lax.broadcasted_iota(jnp.int32, (OWN, 128), 1)
    row = lax.broadcasted_iota(jnp.int32, (OWN, 128), 0)
    for m in range(MEM_SIZE):
        own = slice(m * OWN, (m + 1) * OWN)
        high, low = in_two(table_ref[m * PIECE : m * PIECE + OWN, :])
        tab_ref[own, 0:128] = high
        tab_ref[own, 128:256] = high
        tab_ref[own, 256:384] = low
        tab_ref[own, 384:512] = low
        extra = jnp.broadcast_to(table_ref[m * PIECE + OWN : (m + 1) * PIECE, :], (OWN, 128))
        for k in range(2):
            column = jnp.sum(jnp.where(lane == row + k * OWN, extra, 0.0), axis=1, keepdims=True)
            off_ref[own, k * 128 : (k + 1) * 128] = jnp.broadcast_to(column, (OWN, 128))
    for t in range(n // TILE):
        rows = slice(t * TILE, (t + 1) * TILE)
        slot = t % 2
        feats = feat_ref[:, rows]
        cross = jnp.dot(
            tab_ref[...], jnp.concatenate([feats, feats], axis=0), preferred_element_type=jnp.float32
        )
        virt = virt_ref[:, rows].astype(jnp.float32)
        for h in range(TILE // 128):
            half = slice(h * 128, (h + 1) * 128)
            score_ref[slot, :, half] = (cross[:, half] + off_ref[:, :128]) * virt[:, half] + off_ref[:, 128:]
        score = score_ref[slot]
        top = jnp.max(score, axis=0, keepdims=True)
        expd = jnp.exp2(score - top)
        ratio = virt / jnp.sum(expd, axis=0, keepdims=True)
        w = expd * ratio
        high, low = in_two(w)
        w_ref[slot, :, :TILE] = high
        w_ref[slot, :, TILE:] = low
        part = lax.dot_general(
            w_ref[slot],
            jnp.concatenate([feats, feats], axis=1),
            CONTRACT_LANES,
            preferred_element_type=jnp.float32,
        )
        add_up(t, part, w, acc_ref, cnt_ref)
    finish(virt_ref, acc_ref, cnt_ref, out_ref)


def own_parents(copies_ref):
    lane = lax.broadcasted_iota(jnp.int32, (OWN, 128), 1)
    row = lax.broadcasted_iota(jnp.int32, (OWN, 128), 0)
    sums, extra = copies_ref[:OWN, :], copies_ref[OWN:PIECE, :]
    for k in range(1, copies_ref.shape[0] // PIECE):
        sums += copies_ref[k * PIECE : k * PIECE + OWN, :]
        extra += copies_ref[k * PIECE + OWN : (k + 1) * PIECE, :]
    wide = jnp.broadcast_to(extra, (OWN, 128))
    mass = jnp.sum(jnp.where(lane == row, wide, 0.0), axis=1, keepdims=True) + 1.0
    total = wide[:, OWN : OWN + 1]
    here = jnp.where(lane < D, sums, sums + 1.0) / mass
    there = pltpu.roll(here, D, 1)
    means = jnp.where(lane < D, here, there)
    variances = jnp.where(lane < D, there, here) - means * means
    return lane, row, means, variances, mass / (total + P_SIZE)


def update_kernel(copies_ref, out_ref):
    lane, row, means, variances, weights = own_parents(copies_ref)
    scale = -0.5 / D * LOG2E
    inverse = scale / variances
    table = jnp.where(lane < D, -2.0 * means * inverse, inverse)
    terms = scale * jnp.log(2.0 * math.pi * variances) + means * means * inverse
    offset = jnp.sum(jnp.where(lane < D, terms, 0.0), axis=1, keepdims=True)
    spread = jnp.where(lane == row, offset, jnp.where(lane == row + OWN, LOG2E * jnp.log(weights), 0.0))
    extra = jnp.sum(spread, axis=0, keepdims=True)
    for m in range(MEM_SIZE):
        out_ref[m * PIECE : m * PIECE + OWN, :] = table
        out_ref[m * PIECE + OWN : (m + 1) * PIECE, :] = extra


def last_kernel(copies_ref, mean_ref, var_ref, weight_ref):
    lane, row, means, variances, weights = own_parents(copies_ref)
    mean_ref[...] = means[:, :D]
    var_ref[...] = variances[:, :D]
    weight_ref[...] = jnp.sum(jnp.where(lane == row, weights, 0.0), axis=0, keepdims=True)[:, :OWN]


def vmem(k):
    return [pl.BlockSpec(memory_space=pltpu.VMEM)] * k


def call(kernel, out_shape, scratch_shapes, name, *args, space=pltpu.VMEM, **kw):
    many = isinstance(out_shape, tuple)
    if space is pltpu.HBM:
        args = [pltpu.with_memory_space_constraint(a, space) for a in args]
    return pl.pallas_call(
        kernel,
        out_shape=out_shape,
        in_specs=[pl.BlockSpec(memory_space=space)] * len(args),
        out_specs=tuple(vmem(len(out_shape))) if many else vmem(1)[0],
        scratch_shapes=scratch_shapes,
        compiler_params=pltpu.CompilerParams(vmem_limit_bytes=20 << 20),
        name=name,
        **kw,
    )(*args)


def first_statistics(means, variances, virt, labels, **kw):
    n = means.shape[1]
    return call(
        first_kernel,
        (pltpu.VMEM((256, n), jnp.bfloat16), pltpu.VMEM((MEM_SIZE * PIECE, 128), jnp.float32)),
        [
            pltpu.VMEM((D, n), jnp.float32),
            pltpu.VMEM((D, n), jnp.float32),
            pltpu.VMEM((1, n), jnp.int32),
            pltpu.VMEM((1, n), jnp.int32),
            pltpu.VMEM((P_SIZE, 256), jnp.float32),
            pltpu.VMEM((P_SIZE, 128), jnp.float32),
            pltpu.SemaphoreType.DMA((4,)),
        ],
        "first",
        means,
        variances,
        virt,
        labels,
        space=pltpu.HBM,
        **kw,
    )


def step_statistics(table, feats, virt, **kw):
    return call(
        step_kernel,
        pltpu.VMEM((MEM_SIZE * PIECE, 128), jnp.float32),
        [
            pltpu.VMEM((P_SIZE, 512), jnp.bfloat16),
            pltpu.VMEM((P_SIZE, 256), jnp.float32),
            pltpu.VMEM((2, P_SIZE, TILE), jnp.float32),
            pltpu.VMEM((2, P_SIZE, 2 * TILE), jnp.bfloat16),
            pltpu.VMEM((P_SIZE, 256), jnp.float32),
            pltpu.VMEM((P_SIZE, 128), jnp.float32),
        ],
        "step",
        table,
        feats,
        virt,
        **kw,
    )


def reduce_own(pieces):
    size = lax.axis_size("grp")
    arrived = lax.all_to_all(pieces.reshape(MEM_SIZE, 1, PIECE * 128), MEM, 0, 0, tiled=True)
    shared = jnp.sum(arrived, axis=0, keepdims=True)
    copies = lax.all_to_all(
        jnp.broadcast_to(shared, (size, 1, PIECE * 128)), "grp", 0, 0, tiled=True
    )
    return copies.reshape(size * PIECE, 128)


def next_table(copies, **kw):
    out = call(update_kernel, pltpu.VMEM((MEM_SIZE * PIECE, 128), jnp.float32), [], "update", copies, **kw)
    gathered = lax.all_to_all(out.reshape(MEM_SIZE, 1, PIECE * 128), MEM, 0, 0, tiled=True)
    return gathered.reshape(MEM_SIZE * PIECE, 128)


def final_parents(copies, **kw):
    f32 = jnp.float32
    shapes = (
        jax.ShapeDtypeStruct((OWN, D), f32),
        jax.ShapeDtypeStruct((OWN, D), f32),
        jax.ShapeDtypeStruct((1, OWN), f32),
    )
    means, variances, weights = call(last_kernel, shapes, [], "last", copies, **kw)
    return means, variances, weights.reshape(OWN)


def shards(child_means, child_variances, virtual_counts, assignment):
    virt = virtual_counts.reshape(1, -1)
    feats, pieces = first_statistics(
        child_means.T, child_variances.T, virt, assignment.reshape(1, -1)
    )
    for iteration in range(ITERS):
        pieces = step_statistics(next_table(reduce_own(pieces)), feats, virt)
    return final_parents(reduce_own(pieces))


def solution(mesh):
    split = Mesh(
        mesh.devices.reshape(mesh.shape["grp"], 4, 4, 2), ("grp", "mem_0", "mem_1", "mem_2")
    )
    return jax.shard_map(
        shards,
        mesh=split,
        in_specs=(P(GRP_MEM, None), P(GRP_MEM, None), P(GRP_MEM), P(GRP_MEM, None)),
        out_specs=(P(MEM, None), P(MEM, None), P(MEM)),
        check_vma=False,
    )
```

time: 132 us -> 116 us (0.88)
  local copies, waits for them, and re-layouts: 6.13 us -> 0.12 us
  Pallas kernels: 14.4 us -> 9.84 us
  other arithmetic: 2.61 us -> 0.51 us
  between operations: 2.68 us -> 0.7 us
    pallas_call x3 -> x6, Pallas kernels: 14.4 us -> 9.84 us  [call(): pl.pallas_call(kernel, out_shape=out_shape, in_specs=[pl.BlockSpec(memory...]
    unnamed x4 -> x2, local copies, waits for them, and re-layouts: 3.8 us -> 0.01 us
    slice x6 -> x0, local copies, waits for them, and re-layouts: 1.75 us -> none  [the longest x3 1.74 us: maximize(): total = own[OWN * 128 + OWN]]
where the time goes in v2:
time: 116 us
  blocking collectives  105 us (91%)
  Pallas kernels  9.84 us (8%)
    all_to_all x3, blocking collectives, reduce_own(): lax.all_to_all(pieces.reshape(MEM_SIZE, 1, PIECE * 128), MEM, 0, 0, tiled...  42.6 us
    all_to_all x3, blocking collectives, reduce_own(): lax.all_to_all(jnp.broadcast_to(shared, (size, 1, PIECE * 128)), 'grp', 0...  34.4 us
    all_to_all x2, blocking collectives, next_table(): lax.all_to_all(out.reshape(MEM_SIZE, 1, PIECE * 128), MEM, 0, 0, tiled=True)  27.9 us
    pallas_call x6, Pallas kernels, call(): pl.pallas_call(kernel, out_shape=out_shape, in_specs=[pl.BlockSpec(memory...  9.84 us

profile of v2, /device:TPU:1, one launch (start us, length us, event | category | flops | bytes accessed | tf_op | source)
XLA Modules:
  0.0 116.0 jit_solution(17545995884673181985)
XLA Ops:
  0.6 2.5 %first.1 = (bf16[256,2048]{1,0:T(8,128)(2,1)S(1)}, f32[544,128]{1,0:T(8,128)S(1)}) custom-call(f32[64,2048]{1,0:T(8,128)} %bitcast.28, f32[64,2048]{1,0:T(8,128)} %bitcast.29, s32[1,2048]{1,0:T(1,128)} %bitcast.25, s32[1,2048]{1,0:T(1,128)} %bitcast.30), custom_call_target="tpu_custom_call" | custom-call | tf_op jit(solution)/shard_map/first/pallas_call | solution.py:186
  3.2 17.4 %all_to_all.40 = f32[32,1,2176]{2,1,0:T(1,128)S(1)} all-to-all(f32[32,1,2176]{2,1,0:T(1,128)S(1)} %bitcast.21), channel_id=1, replica_groups=mesh['grp'=8,'mem_0'=4,'mem_1'=4,'mem_2'=2] {'mem_0','mem_1','mem_2'}, dimensions={0} | all-to-all | bytes 557056 | tf_op jit(solution)/shard_map/all_to_all | solution.py:244
  20.6 0.2 reduce_sum.27
  20.8 15.2 %all_to_all.41 = f32[8,1,2176]{2,1,0:T(1,128)S(1)} all-to-all(f32[8,1,2176]{2,1,0:T(1,128)S(1)} %broadcast_in_dim.6), channel_id=1, replica_groups=mesh['grp'=8,'mem_0'=4,'mem_1'=4,'mem_2'=2] {'grp'}, dimensions={0} | all-to-all | bytes 139264 | tf_op jit(solution)/shard_map/all_to_all | solution.py:246
  35.9 0.3 update.2
  36.2 0.0 copy-start
  36.2 14.1 %all_to_all.42 = f32[32,1,2176]{2,1,0:T(1,128)S(1)} all-to-all(f32[32,1,2176]{2,1,0:T(1,128)S(1)} %bitcast.19), channel_id=1, replica_groups=mesh['grp'=8,'mem_0'=4,'mem_1'=4,'mem_2'=2] {'mem_0','mem_1','mem_2'}, dimensions={0} | all-to-all | bytes 557056 | tf_op jit(solution)/shard_map/all_to_all | solution.py:254
  50.3 0.0 copy-done
  50.3 3.0 %step.2 = f32[544,128]{1,0:T(8,128)S(1)} custom-call(f32[544,128]{1,0:T(8,128)S(1)} %bitcast.15, bf16[256,2048]{1,0:T(8,128)(2,1)S(1)} %get-tuple-element.9.feat_ref, s32[1,2048]{1,0:T(1,128)S(1)} %bitcast.26), custom_call_target="tpu_custom_call" | custom-call | tf_op jit(solution)/shard_map/step/pallas_call | solution.py:186
  53.3 12.6 %all_to_all.43 = f32[32,1,2176]{2,1,0:T(1,128)S(1)} all-to-all(f32[32,1,2176]{2,1,0:T(1,128)S(1)} %bitcast.18), channel_id=1, replica_groups=mesh['grp'=8,'mem_0'=4,'mem_1'=4,'mem_2'=2] {'mem_0','mem_1','mem_2'}, dimensions={0} | all-to-all | bytes 557056 | tf_op jit(solution)/shard_map/all_to_all | solution.py:244
  65.9 0.2 reduce_sum.28
  66.1 9.6 %all_to_all.44 = f32[8,1,2176]{2,1,0:T(1,128)S(1)} all-to-all(f32[8,1,2176]{2,1,0:T(1,128)S(1)} %broadcast_in_dim.7), channel_id=1, replica_groups=mesh['grp'=8,'mem_0'=4,'mem_1'=4,'mem_2'=2] {'grp'}, dimensions={0} | all-to-all | bytes 139264 | tf_op jit(solution)/shard_map/all_to_all | solution.py:246
  75.7 0.3 update.3
  76.0 13.8 %all_to_all.45 = f32[32,1,2176]{2,1,0:T(1,128)S(1)} all-to-all(f32[32,1,2176]{2,1,0:T(1,128)S(1)} %bitcast.20), channel_id=1, replica_groups=mesh['grp'=8,'mem_0'=4,'mem_1'=4,'mem_2'=2] {'mem_0','mem_1','mem_2'}, dimensions={0} | all-to-all | bytes 557056 | tf_op jit(solution)/shard_map/all_to_all | solution.py:254
  89.8 3.0 %step.3 = f32[544,128]{1,0:T(8,128)S(1)} custom-call(f32[544,128]{1,0:T(8,128)S(1)} %bitcast.16, bf16[256,2048]{1,0:T(8,128)(2,1)S(1)} %get-tuple-element.9.feat_ref, s32[1,2048]{1,0:T(1,128)S(1)} %bitcast.27), custom_call_target="tpu_custom_call" | custom-call | tf_op jit(solution)/shard_map/step/pallas_call | solution.py:186
  92.8 12.6 %all_to_all.46 = f32[32,1,2176]{2,1,0:T(1,128)S(1)} all-to-all(f32[32,1,2176]{2,1,0:T(1,128)S(1)} %bitcast.17), channel_id=1, replica_groups=mesh['grp'=8,'mem_0'=4,'mem_1'=4,'mem_2'=2] {'mem_0','mem_1','mem_2'}, dimensions={0} | all-to-all | bytes 557056 | tf_op jit(solution)/shard_map/all_to_all | solution.py:244
  105.4 0.2 reduce_sum.29
  105.6 9.6 %all_to_all.47 = f32[8,1,2176]{2,1,0:T(1,128)S(1)} all-to-all(f32[8,1,2176]{2,1,0:T(1,128)S(1)} %broadcast_in_dim.8), channel_id=1, replica_groups=mesh['grp'=8,'mem_0'=4,'mem_1'=4,'mem_2'=2] {'grp'}, dimensions={0} | all-to-all | bytes 139264 | tf_op jit(solution)/shard_map/all_to_all | solution.py:246
  115.2 0.8 last.1
  (3 shorter events, 0.1 us)
Async XLA Ops:
  36.2 14.1 %copy-start = (s32[2048]{0:T(1024)S(1)}, s32[2048]{0:T(1024)}, u32[]{:S(2)}) copy-start(s32[2048]{0:T(1024)} %param.6) | copy-start | bytes 24580

commit v3 on v2

--- a/solution.py
+++ b/solution.py
@@ -15,8 +15,12 @@
 OWN = P_SIZE // MEM_SIZE
 PIECE = OWN + 1
 TILE = 256
-GRP_MEM = ("grp", "mem_0", "mem_1", "mem_2")
-MEM = ("mem_0", "mem_1", "mem_2")
+BOTH = ("grp", "mem")
+LINE = (2, 0, 1, 3)
+MEM_START = 2 * 8 + 2 * 2 + 1
+MEM_LIST = [8 * y + 2 * x + core for y in LINE for x in LINE for core in (0, 1)]
+MEM_ORDER = MEM_LIST[MEM_LIST.index(MEM_START) :] + MEM_LIST[: MEM_LIST.index(MEM_START)]
+GRP_ORDER = [4, 0, 3, 7, 2, 6, 1, 5]
 LOG2E = math.log2(math.e)
 CONTRACT_LANES = (((1,), (1,)), ((), ()))
 
@@ -30,12 +34,12 @@
     lane = lax.broadcasted_iota(jnp.int32, (OWN, 128), 1)
     row = lax.broadcasted_iota(jnp.int32, (OWN, 128), 0)
     last = lax.broadcasted_iota(jnp.int32, (1, 128), 1) == OWN
-    for m in range(MEM_SIZE):
+    for k, m in enumerate(MEM_ORDER):
         own = slice(m * OWN, (m + 1) * OWN)
-        out_ref[m * PIECE : m * PIECE + OWN, :] = sums[own]
+        out_ref[k * PIECE : k * PIECE + OWN, :] = sums[own]
         spread = jnp.where(lane == row, counts[own], 0.0)
         flat = jnp.sum(spread, axis=0, keepdims=True)
-        out_ref[m * PIECE + OWN : (m + 1) * PIECE, :] = jnp.where(last, local_total, flat)
+        out_ref[k * PIECE + OWN : (k + 1) * PIECE, :] = jnp.where(last, local_total, flat)
 
 
 def first_kernel(
@@ -97,17 +101,17 @@
     n = feat_ref.shape[1]
     lane = lax.broadcasted_iota(jnp.int32, (OWN, 128), 1)
     row = lax.broadcasted_iota(jnp.int32, (OWN, 128), 0)
-    for m in range(MEM_SIZE):
+    for k, m in enumerate(MEM_ORDER):
         own = slice(m * OWN, (m + 1) * OWN)
-        high, low = in_two(table_ref[m * PIECE : m * PIECE + OWN, :])
+        high, low = in_two(table_ref[k * PIECE : k * PIECE + OWN, :])
         tab_ref[own, 0:128] = high
         tab_ref[own, 128:256] = high
         tab_ref[own, 256:384] = low
         tab_ref[own, 384:512] = low
-        extra = jnp.broadcast_to(table_ref[m * PIECE + OWN : (m + 1) * PIECE, :], (OWN, 128))
-        for k in range(2):
-            column = jnp.sum(jnp.where(lane == row + k * OWN, extra, 0.0), axis=1, keepdims=True)
-            off_ref[own, k * 128 : (k + 1) * 128] = jnp.broadcast_to(column, (OWN, 128))
+        extra = jnp.broadcast_to(table_ref[k * PIECE + OWN : (k + 1) * PIECE, :], (OWN, 128))
+        for j in range(2):
+            column = jnp.sum(jnp.where(lane == row + j * OWN, extra, 0.0), axis=1, keepdims=True)
+            off_ref[own, j * 128 : (j + 1) * 128] = jnp.broadcast_to(column, (OWN, 128))
     for t in range(n // TILE):
         rows = slice(t * TILE, (t + 1) * TILE)
         slot = t % 2
@@ -239,19 +243,21 @@
     )
 
 
+def exchange(pieces, axis, order):
+    return lax.all_to_all(pieces, axis, 0, 0, axis_index_groups=[order], tiled=True)
+
+
 def reduce_own(pieces):
-    size = lax.axis_size("grp")
-    arrived = lax.all_to_all(pieces.reshape(MEM_SIZE, 1, PIECE * 128), MEM, 0, 0, tiled=True)
+    size = len(GRP_ORDER)
+    arrived = exchange(pieces.reshape(MEM_SIZE, 1, PIECE * 128), "mem", MEM_ORDER)
     shared = jnp.sum(arrived, axis=0, keepdims=True)
-    copies = lax.all_to_all(
-        jnp.broadcast_to(shared, (size, 1, PIECE * 128)), "grp", 0, 0, tiled=True
-    )
+    copies = exchange(jnp.broadcast_to(shared, (size, 1, PIECE * 128)), "grp", GRP_ORDER)
     return copies.reshape(size * PIECE, 128)
 
 
 def next_table(copies, **kw):
     out = call(update_kernel, pltpu.VMEM((MEM_SIZE * PIECE, 128), jnp.float32), [], "update", copies, **kw)
-    gathered = lax.all_to_all(out.reshape(MEM_SIZE, 1, PIECE * 128), MEM, 0, 0, tiled=True)
+    gathered = exchange(out.reshape(MEM_SIZE, 1, PIECE * 128), "mem", MEM_ORDER)
     return gathered.reshape(MEM_SIZE * PIECE, 128)
 
 
@@ -277,13 +283,10 @@
 
 
 def solution(mesh):
-    split = Mesh(
-        mesh.devices.reshape(mesh.shape["grp"], 4, 4, 2), ("grp", "mem_0", "mem_1", "mem_2")
-    )
     return jax.shard_map(
         shards,
-        mesh=split,
-        in_specs=(P(GRP_MEM, None), P(GRP_MEM, None), P(GRP_MEM), P(GRP_MEM, None)),
-        out_specs=(P(MEM, None), P(MEM, None), P(MEM)),
+        mesh=mesh,
+        in_specs=(P(BOTH, None), P(BOTH, None), P(BOTH), P(BOTH, None)),
+        out_specs=(P("mem", None), P("mem", None), P("mem")),
         check_vma=False,
     )

time: 116 us -> 106 us (0.914)
  blocking collectives: 105 us -> 94.6 us
    all_to_all x8, blocking collectives: 105 us -> 94.6 us  [exchange(): lax.all_to_all(pieces, axis, 0, 0, axis_index_groups=[order], tiled=True)]
where the time goes in v3:
time: 106 us
  blocking collectives  94.6 us (89%)
  Pallas kernels  9.83 us (9%)
    all_to_all x8, blocking collectives, exchange(): lax.all_to_all(pieces, axis, 0, 0, axis_index_groups=[order], tiled=True)  94.6 us
    pallas_call x6, Pallas kernels, call(): pl.pallas_call(kernel, out_shape=out_shape, in_specs=[pl.BlockSpec(memory...  9.83 us

profile of v3, /device:TPU:1, one launch (start us, length us, event | category | flops | bytes accessed | tf_op | source)
XLA Modules:
  0.0 105.8 jit_solution(9324454776509472179)
XLA Ops:
  0.6 2.5 %first.1 = (bf16[256,2048]{1,0:T(8,128)(2,1)S(1)}, f32[544,128]{1,0:T(8,128)S(1)}) custom-call(f32[64,2048]{1,0:T(8,128)} %bitcast.28, f32[64,2048]{1,0:T(8,128)} %bitcast.29, s32[1,2048]{1,0:T(1,128)} %bitcast.25, s32[1,2048]{1,0:T(1,128)} %bitcast.30), custom_call_target="tpu_custom_call" | custom-call | tf_op jit(solution)/shard_map/first/pallas_call | solution.py:190
  3.2 14.1 %all_to_all.40 = f32[32,1,2176]{2,1,0:T(1,128)S(1)} all-to-all(f32[32,1,2176]{2,1,0:T(1,128)S(1)} %bitcast.21), channel_id=1, replica_groups={{21,16,17,18,19,22,23,4,5,0,1,2,3,6,7,12,13,8,9,10,11,14,15,28,29,24,25..., dimensions={0} | all-to-all | bytes 557056 | tf_op jit(solution)/shard_map/all_to_all | solution.py:247
  17.2 0.2 reduce_sum.27
  17.4 11.9 %all_to_all.41 = f32[8,1,2176]{2,1,0:T(1,128)S(1)} all-to-all(f32[8,1,2176]{2,1,0:T(1,128)S(1)} %broadcast_in_dim.6), channel_id=1, replica_groups={{128,0,96,224,64,192,32,160},{129,1,97,225,65,193,33,161},{130,2,98,226..., dimensions={0} | all-to-all | bytes 139264 | tf_op jit(solution)/shard_map/all_to_all | solution.py:247
  29.4 0.3 update.2
  29.7 0.0 copy-start
  29.7 13.0 %all_to_all.42 = f32[32,1,2176]{2,1,0:T(1,128)S(1)} all-to-all(f32[32,1,2176]{2,1,0:T(1,128)S(1)} %bitcast.19), channel_id=1, replica_groups={{21,16,17,18,19,22,23,4,5,0,1,2,3,6,7,12,13,8,9,10,11,14,15,28,29,24,25..., dimensions={0} | all-to-all | bytes 557056 | tf_op jit(solution)/shard_map/all_to_all | solution.py:247
  42.7 0.0 copy-done
  42.7 3.0 %step.2 = f32[544,128]{1,0:T(8,128)S(1)} custom-call(f32[544,128]{1,0:T(8,128)S(1)} %bitcast.15, bf16[256,2048]{1,0:T(8,128)(2,1)S(1)} %get-tuple-element.9.feat_ref, s32[1,2048]{1,0:T(1,128)S(1)} %bitcast.26), custom_call_target="tpu_custom_call" | custom-call | tf_op jit(solution)/shard_map/step/pallas_call | solution.py:190
  45.7 11.9 %all_to_all.43 = f32[32,1,2176]{2,1,0:T(1,128)S(1)} all-to-all(f32[32,1,2176]{2,1,0:T(1,128)S(1)} %bitcast.18), channel_id=1, replica_groups={{21,16,17,18,19,22,23,4,5,0,1,2,3,6,7,12,13,8,9,10,11,14,15,28,29,24,25..., dimensions={0} | all-to-all | bytes 557056 | tf_op jit(solution)/shard_map/all_to_all | solution.py:247
  57.6 0.2 reduce_sum.28
  57.8 9.6 %all_to_all.44 = f32[8,1,2176]{2,1,0:T(1,128)S(1)} all-to-all(f32[8,1,2176]{2,1,0:T(1,128)S(1)} %broadcast_in_dim.7), channel_id=1, replica_groups={{128,0,96,224,64,192,32,160},{129,1,97,225,65,193,33,161},{130,2,98,226..., dimensions={0} | all-to-all | bytes 139264 | tf_op jit(solution)/shard_map/all_to_all | solution.py:247
  67.4 0.3 update.3
  67.7 12.7 %all_to_all.45 = f32[32,1,2176]{2,1,0:T(1,128)S(1)} all-to-all(f32[32,1,2176]{2,1,0:T(1,128)S(1)} %bitcast.20), channel_id=1, replica_groups={{21,16,17,18,19,22,23,4,5,0,1,2,3,6,7,12,13,8,9,10,11,14,15,28,29,24,25..., dimensions={0} | all-to-all | bytes 557056 | tf_op jit(solution)/shard_map/all_to_all | solution.py:247
  80.4 3.0 %step.3 = f32[544,128]{1,0:T(8,128)S(1)} custom-call(f32[544,128]{1,0:T(8,128)S(1)} %bitcast.16, bf16[256,2048]{1,0:T(8,128)(2,1)S(1)} %get-tuple-element.9.feat_ref, s32[1,2048]{1,0:T(1,128)S(1)} %bitcast.27), custom_call_target="tpu_custom_call" | custom-call | tf_op jit(solution)/shard_map/step/pallas_call | solution.py:190
  83.4 11.9 %all_to_all.46 = f32[32,1,2176]{2,1,0:T(1,128)S(1)} all-to-all(f32[32,1,2176]{2,1,0:T(1,128)S(1)} %bitcast.17), channel_id=1, replica_groups={{21,16,17,18,19,22,23,4,5,0,1,2,3,6,7,12,13,8,9,10,11,14,15,28,29,24,25..., dimensions={0} | all-to-all | bytes 557056 | tf_op jit(solution)/shard_map/all_to_all | solution.py:247
  95.3 0.2 reduce_sum.29
  95.5 9.5 %all_to_all.47 = f32[8,1,2176]{2,1,0:T(1,128)S(1)} all-to-all(f32[8,1,2176]{2,1,0:T(1,128)S(1)} %broadcast_in_dim.8), channel_id=1, replica_groups={{128,0,96,224,64,192,32,160},{129,1,97,225,65,193,33,161},{130,2,98,226..., dimensions={0} | all-to-all | bytes 139264 | tf_op jit(solution)/shard_map/all_to_all | solution.py:247
  105.0 0.8 last.1
  (3 shorter events, 0.1 us)
Async XLA Ops:
  29.7 13.0 %copy-start = (s32[2048]{0:T(1024)S(1)}, s32[2048]{0:T(1024)}, u32[]{:S(2)}) copy-start(s32[2048]{0:T(1024)} %param.6) | copy-start | bytes 24580

commit v4 on v3

--- a/solution.py
+++ b/solution.py
@@ -16,11 +16,12 @@
 PIECE = OWN + 1
 TILE = 256
 BOTH = ("grp", "mem")
-LINE = (2, 0, 1, 3)
+Y_LINE = (2, 0, 3, 1)
+X_LINE = (2, 0, 1, 3)
 MEM_START = 2 * 8 + 2 * 2 + 1
-MEM_LIST = [8 * y + 2 * x + core for y in LINE for x in LINE for core in (0, 1)]
+MEM_LIST = [8 * y + 2 * x + core for y in Y_LINE for x in X_LINE for core in (0, 1)]
 MEM_ORDER = MEM_LIST[MEM_LIST.index(MEM_START) :] + MEM_LIST[: MEM_LIST.index(MEM_START)]
-GRP_ORDER = [4, 0, 3, 7, 2, 6, 1, 5]
+GRP_ORDER = [4, 0, 7, 3, 6, 2, 5, 1]
 LOG2E = math.log2(math.e)
 CONTRACT_LANES = (((1,), (1,)), ((), ()))
 

time: 106 us -> 106 us (level)
  no operation moved by 1% of the time
where the time goes in v4:
time: 106 us; the launch traced here: 105 us
  blocking collectives  94 us (89%)
  Pallas kernels  9.83 us (9%)
    all_to_all x8, blocking collectives, exchange(): lax.all_to_all(pieces, axis, 0, 0, axis_index_groups=[order], tiled=True)  94 us
    pallas_call x6, Pallas kernels, call(): pl.pallas_call(kernel, out_shape=out_shape, in_specs=[pl.BlockSpec(memory...  9.83 us

profile of v4, /device:TPU:1, one launch (start us, length us, event | category | flops | bytes accessed | tf_op | source)
XLA Modules:
  0.0 105.1 jit_solution(755664859410402350)
XLA Ops:
  0.6 2.5 %first.1 = (bf16[256,2048]{1,0:T(8,128)(2,1)S(1)}, f32[544,128]{1,0:T(8,128)S(1)}) custom-call(f32[64,2048]{1,0:T(8,128)} %bitcast.28, f32[64,2048]{1,0:T(8,128)} %bitcast.29, s32[1,2048]{1,0:T(1,128)} %bitcast.25, s32[1,2048]{1,0:T(1,128)} %bitcast.30), custom_call_target="tpu_custom_call" | custom-call | tf_op jit(solution)/shard_map/first/pallas_call | solution.py:191
  3.2 14.2 %all_to_all.40 = f32[32,1,2176]{2,1,0:T(1,128)S(1)} all-to-all(f32[32,1,2176]{2,1,0:T(1,128)S(1)} %bitcast.21), channel_id=1, replica_groups={{21,16,17,18,19,22,23,4,5,0,1,2,3,6,7,28,29,24,25,26,27,30,31,12,13,8,9..., dimensions={0} | all-to-all | bytes 557056 | tf_op jit(solution)/shard_map/all_to_all | solution.py:248
  17.4 0.2 reduce_sum.27
  17.6 11.9 %all_to_all.41 = f32[8,1,2176]{2,1,0:T(1,128)S(1)} all-to-all(f32[8,1,2176]{2,1,0:T(1,128)S(1)} %broadcast_in_dim.6), channel_id=1, replica_groups={{128,0,224,96,192,64,160,32},{129,1,225,97,193,65,161,33},{130,2,226,98..., dimensions={0} | all-to-all | bytes 139264 | tf_op jit(solution)/shard_map/all_to_all | solution.py:248
  29.5 0.3 update.2
  29.8 0.0 copy-start
  29.8 12.8 %all_to_all.42 = f32[32,1,2176]{2,1,0:T(1,128)S(1)} all-to-all(f32[32,1,2176]{2,1,0:T(1,128)S(1)} %bitcast.19), channel_id=1, replica_groups={{21,16,17,18,19,22,23,4,5,0,1,2,3,6,7,28,29,24,25,26,27,30,31,12,13,8,9..., dimensions={0} | all-to-all | bytes 557056 | tf_op jit(solution)/shard_map/all_to_all | solution.py:248
  42.7 0.0 copy-done
  42.7 3.0 %step.2 = f32[544,128]{1,0:T(8,128)S(1)} custom-call(f32[544,128]{1,0:T(8,128)S(1)} %bitcast.15, bf16[256,2048]{1,0:T(8,128)(2,1)S(1)} %get-tuple-element.9.feat_ref, s32[1,2048]{1,0:T(1,128)S(1)} %bitcast.26), custom_call_target="tpu_custom_call" | custom-call | tf_op jit(solution)/shard_map/step/pallas_call | solution.py:191
  45.7 11.9 %all_to_all.43 = f32[32,1,2176]{2,1,0:T(1,128)S(1)} all-to-all(f32[32,1,2176]{2,1,0:T(1,128)S(1)} %bitcast.18), channel_id=1, replica_groups={{21,16,17,18,19,22,23,4,5,0,1,2,3,6,7,28,29,24,25,26,27,30,31,12,13,8,9..., dimensions={0} | all-to-all | bytes 557056 | tf_op jit(solution)/shard_map/all_to_all | solution.py:248
  57.5 0.2 reduce_sum.28
  57.7 9.3 %all_to_all.44 = f32[8,1,2176]{2,1,0:T(1,128)S(1)} all-to-all(f32[8,1,2176]{2,1,0:T(1,128)S(1)} %broadcast_in_dim.7), channel_id=1, replica_groups={{128,0,224,96,192,64,160,32},{129,1,225,97,193,65,161,33},{130,2,226,98..., dimensions={0} | all-to-all | bytes 139264 | tf_op jit(solution)/shard_map/all_to_all | solution.py:248
  67.0 0.3 update.3
  67.3 12.8 %all_to_all.45 = f32[32,1,2176]{2,1,0:T(1,128)S(1)} all-to-all(f32[32,1,2176]{2,1,0:T(1,128)S(1)} %bitcast.20), channel_id=1, replica_groups={{21,16,17,18,19,22,23,4,5,0,1,2,3,6,7,28,29,24,25,26,27,30,31,12,13,8,9..., dimensions={0} | all-to-all | bytes 557056 | tf_op jit(solution)/shard_map/all_to_all | solution.py:248
  80.1 3.0 %step.3 = f32[544,128]{1,0:T(8,128)S(1)} custom-call(f32[544,128]{1,0:T(8,128)S(1)} %bitcast.16, bf16[256,2048]{1,0:T(8,128)(2,1)S(1)} %get-tuple-element.9.feat_ref, s32[1,2048]{1,0:T(1,128)S(1)} %bitcast.27), custom_call_target="tpu_custom_call" | custom-call | tf_op jit(solution)/shard_map/step/pallas_call | solution.py:191
  83.1 11.9 %all_to_all.46 = f32[32,1,2176]{2,1,0:T(1,128)S(1)} all-to-all(f32[32,1,2176]{2,1,0:T(1,128)S(1)} %bitcast.17), channel_id=1, replica_groups={{21,16,17,18,19,22,23,4,5,0,1,2,3,6,7,28,29,24,25,26,27,30,31,12,13,8,9..., dimensions={0} | all-to-all | bytes 557056 | tf_op jit(solution)/shard_map/all_to_all | solution.py:248
  94.9 0.2 reduce_sum.29
  95.2 9.2 %all_to_all.47 = f32[8,1,2176]{2,1,0:T(1,128)S(1)} all-to-all(f32[8,1,2176]{2,1,0:T(1,128)S(1)} %broadcast_in_dim.8), channel_id=1, replica_groups={{128,0,224,96,192,64,160,32},{129,1,225,97,193,65,161,33},{130,2,226,98..., dimensions={0} | all-to-all | bytes 139264 | tf_op jit(solution)/shard_map/all_to_all | solution.py:248
  104.3 0.8 last.1
  (3 shorter events, 0.1 us)
Async XLA Ops:
  29.8 12.8 %copy-start = (s32[2048]{0:T(1024)S(1)}, s32[2048]{0:T(1024)}, u32[]{:S(2)}) copy-start(s32[2048]{0:T(1024)} %param.6) | copy-start | bytes 24580

commit v5 on v4

--- a/solution.py
+++ b/solution.py
@@ -159,6 +159,18 @@
     return lane, row, means, variances, mass / (total + P_SIZE)
 
 
+def share_kernel(arrived_ref, out_ref):
+    parts = [[], []]
+    for k in range(MEM_SIZE):
+        parts[0].append(arrived_ref[k * PIECE : k * PIECE + OWN, :])
+        parts[1].append(arrived_ref[k * PIECE + OWN : (k + 1) * PIECE, :])
+    while len(parts[0]) > 1:
+        parts = [[a + b for a, b in zip(p[::2], p[1::2])] for p in parts]
+    for k in range(len(GRP_ORDER)):
+        out_ref[k * PIECE : k * PIECE + OWN, :] = parts[0][0]
+        out_ref[k * PIECE + OWN : (k + 1) * PIECE, :] = parts[1][0]
+
+
 def update_kernel(copies_ref, out_ref):
     lane, row, means, variances, weights = own_parents(copies_ref)
     scale = -0.5 / D * LOG2E
@@ -251,8 +263,14 @@
 def reduce_own(pieces):
     size = len(GRP_ORDER)
     arrived = exchange(pieces.reshape(MEM_SIZE, 1, PIECE * 128), "mem", MEM_ORDER)
-    shared = jnp.sum(arrived, axis=0, keepdims=True)
-    copies = exchange(jnp.broadcast_to(shared, (size, 1, PIECE * 128)), "grp", GRP_ORDER)
+    shared = call(
+        share_kernel,
+        pltpu.VMEM((size * PIECE, 128), jnp.float32),
+        [],
+        "share",
+        arrived.reshape(MEM_SIZE * PIECE, 128),
+    )
+    copies = exchange(shared.reshape(size, 1, PIECE * 128), "grp", GRP_ORDER)
     return copies.reshape(size * PIECE, 128)
 
 

time: 106 us -> 105 us (level)
    pallas_call x6 -> x9, Pallas kernels: 9.83 us -> 9.93 us  [call(): pl.pallas_call(kernel, out_shape=out_shape, in_specs=[pl.BlockSpec(memory...]
where the time goes in v5:
time: 105 us
  blocking collectives  94 us (90%)
  Pallas kernels  9.93 us (9%)
    all_to_all x8, blocking collectives, exchange(): lax.all_to_all(pieces, axis, 0, 0, axis_index_groups=[order], tiled=True)  94 us
    pallas_call x9, Pallas kernels, call(): pl.pallas_call(kernel, out_shape=out_shape, in_specs=[pl.BlockSpec(memory...  9.93 us

profile of v5, /device:TPU:1, one launch (start us, length us, event | category | flops | bytes accessed | tf_op | source)
XLA Modules:
  0.0 104.6 jit_solution(7584777797664813491)
XLA Ops:
  0.6 2.5 %first.1 = (bf16[256,2048]{1,0:T(8,128)(2,1)S(1)}, f32[544,128]{1,0:T(8,128)S(1)}) custom-call(f32[64,2048]{1,0:T(8,128)} %bitcast.40, f32[64,2048]{1,0:T(8,128)} %bitcast.41, s32[1,2048]{1,0:T(1,128)} %bitcast.37, s32[1,2048]{1,0:T(1,128)} %bitcast.42), custom_call_target="tpu_custom_call" | custom-call | tf_op jit(solution)/shard_map/first/pallas_call | solution.py:203
  3.2 14.2 %all_to_all.40 = f32[32,1,2176]{2,1,0:T(1,128)S(1)} all-to-all(f32[32,1,2176]{2,1,0:T(1,128)S(1)} %bitcast.30), channel_id=1, replica_groups={{21,16,17,18,19,22,23,4,5,0,1,2,3,6,7,28,29,24,25,26,27,30,31,12,13,8,9..., dimensions={0} | all-to-all | bytes 557056 | tf_op jit(solution)/shard_map/all_to_all | solution.py:260
  17.4 11.9 %all_to_all.41 = f32[8,1,2176]{2,1,0:T(1,128)S(1)} all-to-all(f32[8,1,2176]{2,1,0:T(1,128)S(1)} %bitcast.32), channel_id=1, replica_groups={{128,0,224,96,192,64,160,32},{129,1,225,97,193,65,161,33},{130,2,226,98..., dimensions={0} | all-to-all | bytes 139264 | tf_op jit(solution)/shard_map/all_to_all | solution.py:260
  29.3 0.3 update.2
  29.6 0.0 copy-start
  29.6 12.8 %all_to_all.42 = f32[32,1,2176]{2,1,0:T(1,128)S(1)} all-to-all(f32[32,1,2176]{2,1,0:T(1,128)S(1)} %bitcast.26), channel_id=1, replica_groups={{21,16,17,18,19,22,23,4,5,0,1,2,3,6,7,28,29,24,25,26,27,30,31,12,13,8,9..., dimensions={0} | all-to-all | bytes 557056 | tf_op jit(solution)/shard_map/all_to_all | solution.py:260
  42.5 0.0 copy-done
  42.5 3.0 %step.2 = f32[544,128]{1,0:T(8,128)S(1)} custom-call(f32[544,128]{1,0:T(8,128)S(1)} %bitcast.21, bf16[256,2048]{1,0:T(8,128)(2,1)S(1)} %get-tuple-element.9.feat_ref, s32[1,2048]{1,0:T(1,128)S(1)} %bitcast.38), custom_call_target="tpu_custom_call" | custom-call | tf_op jit(solution)/shard_map/step/pallas_call | solution.py:203
  45.5 11.9 %all_to_all.43 = f32[32,1,2176]{2,1,0:T(1,128)S(1)} all-to-all(f32[32,1,2176]{2,1,0:T(1,128)S(1)} %bitcast.24), channel_id=1, replica_groups={{21,16,17,18,19,22,23,4,5,0,1,2,3,6,7,28,29,24,25,26,27,30,31,12,13,8,9..., dimensions={0} | all-to-all | bytes 557056 | tf_op jit(solution)/shard_map/all_to_all | solution.py:260
  57.4 9.3 %all_to_all.44 = f32[8,1,2176]{2,1,0:T(1,128)S(1)} all-to-all(f32[8,1,2176]{2,1,0:T(1,128)S(1)} %bitcast.34), channel_id=1, replica_groups={{128,0,224,96,192,64,160,32},{129,1,225,97,193,65,161,33},{130,2,226,98..., dimensions={0} | all-to-all | bytes 139264 | tf_op jit(solution)/shard_map/all_to_all | solution.py:260
  66.7 0.3 update.3
  67.0 12.8 %all_to_all.45 = f32[32,1,2176]{2,1,0:T(1,128)S(1)} all-to-all(f32[32,1,2176]{2,1,0:T(1,128)S(1)} %bitcast.28), channel_id=1, replica_groups={{21,16,17,18,19,22,23,4,5,0,1,2,3,6,7,28,29,24,25,26,27,30,31,12,13,8,9..., dimensions={0} | all-to-all | bytes 557056 | tf_op jit(solution)/shard_map/all_to_all | solution.py:260
  79.7 3.0 %step.3 = f32[544,128]{1,0:T(8,128)S(1)} custom-call(f32[544,128]{1,0:T(8,128)S(1)} %bitcast.22, bf16[256,2048]{1,0:T(8,128)(2,1)S(1)} %get-tuple-element.9.feat_ref, s32[1,2048]{1,0:T(1,128)S(1)} %bitcast.39), custom_call_target="tpu_custom_call" | custom-call | tf_op jit(solution)/shard_map/step/pallas_call | solution.py:203
  82.7 11.9 %all_to_all.46 = f32[32,1,2176]{2,1,0:T(1,128)S(1)} all-to-all(f32[32,1,2176]{2,1,0:T(1,128)S(1)} %bitcast.23), channel_id=1, replica_groups={{21,16,17,18,19,22,23,4,5,0,1,2,3,6,7,28,29,24,25,26,27,30,31,12,13,8,9..., dimensions={0} | all-to-all | bytes 557056 | tf_op jit(solution)/shard_map/all_to_all | solution.py:260
  94.6 9.2 %all_to_all.47 = f32[8,1,2176]{2,1,0:T(1,128)S(1)} all-to-all(f32[8,1,2176]{2,1,0:T(1,128)S(1)} %bitcast.36), channel_id=1, replica_groups={{128,0,224,96,192,64,160,32},{129,1,225,97,193,65,161,33},{130,2,226,98..., dimensions={0} | all-to-all | bytes 139264 | tf_op jit(solution)/shard_map/all_to_all | solution.py:260
  103.8 0.8 last.1
  (3 shorter events, 0.1 us)
Async XLA Ops:
  29.6 12.8 %copy-start = (s32[2048]{0:T(1024)S(1)}, s32[2048]{0:T(1024)}, u32[]{:S(2)}) copy-start(s32[2048]{0:T(1024)} %param.6) | copy-start | bytes 24580
